TPU v7x, 32 devices: a whole 2x2x4 slice. The times are simulated.
32 devices in a mesh: cuts: 16 (over z, y, x), circ: 2 (over core).
Axes of the slice: x: 2, y: 2, z: 4, core: 2. Of those that a mesh axis runs over, the one named last changes fastest.
Arguments:
- sources: bfloat16 [16, 8, 2, 16, 1024], P('cuts', None, 'circ'), may hold values from -6 to 6
- block_inverse: bfloat16 [2, 1024, 1024], P('circ'), may hold values from -0.0115625 to 0.92
- memory_factor: float32 [16, 2, 1024], P('cuts', 'circ'), may hold values from 0.5 to 1
- coupling_target: int32 [2, 4], P('circ'), may hold values from 0 to 1, as said below
- coupling_weight: bfloat16 [2, 4, 128, 1024], P('circ'), may hold values from -0.09375 to 0.09375
- coarse_decay: float32 [16, 2, 1024], P('cuts', 'circ'), may hold values from 0.2 to 0.995
- initial_state: float32 [2, 16, 1024], P('circ'), may hold values from -6 to 6
Outputs:
- slice_starts: float32 [16, 2, 16, 1024], P('cuts', 'circ')
- waveform: bfloat16 [16, 8, 2, 16, 1024], P('cuts', None, 'circ')
Inputs may be any that keep to these rules, and one draw needn't show every extreme that they name: `coupling_target`: row j names 4 subcircuits, j itself among them possibly; a row may name one subcircuit twice.
All inputs are finite; a program needn't handle non-finite values.
Results may differ from a plain program's by a relative error of at most 0.007.
Values sent between devices are 32-bit elements; how exact they have to be, the bound alone decides.
A program may use at most 64 MiB of HBM per device.

v0:
```python
import functools

import jax
import jax.numpy as jnp
from jax import lax
from jax.experimental import pallas as pl
from jax.experimental.pallas import tpu as pltpu
from jax.sharding import PartitionSpec as P

SWEEPS = 3
ITERS = 2
MESH = pl.DeviceIdType.MESH
F32 = jnp.float32
BF16 = jnp.bfloat16
LANE = 128


def dot(a, b):
    return jnp.dot(a.astype(BF16), b.astype(BF16), preferred_element_type=F32)


def kernel(
    cuts,
    circ,
    steps,
    src_in,
    inv_in,
    mem_in,
    tgt_in,
    cw_in,
    dec_in,
    init_in,
    start_ref,
    wave_out,
    src_ref,
    inv_ref,
    mem_ref,
    tgt_ref,
    cw_ref,
    dec_ref,
    init_ref,
    wave_ref,
    sem_in,
    sem_out,
    inv_t,
    pow1,
    pow2,
    pow4,
    port_t,
    resp,
    port_resp,
    own,
    free,
    terms_buf,
    gather_buf,
    chain_buf,
    state_buf,
    decay_buf,
    part_buf,
    inflow_buf,
    send1,
    recv1,
    send2,
    recv2,
    send_d,
    recv_d,
    send_x,
    recv_x,
):
    n = lax.axis_index("cuts")
    me = lax.axis_index("circ")
    nodes = inv_ref.shape[0]
    scen = init_ref.shape[0]
    rows = src_ref.shape[0]
    blocks, ports = cw_ref.shape[0], cw_ref.shape[1]
    cols = nodes // LANE
    base = (cuts - cols) // 2
    piece = n - base
    owner = jnp.logical_and(n >= base, n < base + cols)
    lane = pl.multiple_of(piece * LANE, LANE)

    def cut(k):
        return lax.rem(n + k, cuts)

    def peer(k):
        return lax.rem(me + k, circ)

    barrier = pltpu.get_barrier_semaphore()

    @pl.loop(1, cuts)
    def _(k):
        pl.semaphore_signal(barrier, inc=1, device_id=(cut(k), me), device_id_type=MESH)

    for k in range(1, circ):
        pl.semaphore_signal(barrier, inc=1, device_id=(n, peer(k)), device_id_type=MESH)

    pairs = (
        (dec_in, dec_ref),
        (src_in, src_ref),
        (inv_in, inv_ref),
        (mem_in, mem_ref),
        (cw_in, cw_ref),
        (tgt_in, tgt_ref),
        (init_in, init_ref),
    )
    loads = [pltpu.make_async_copy(a, b, sem_in.at[k]) for k, (a, b) in enumerate(pairs)]
    for copy in loads:
        copy.start()

    def term_copy(c, k, dest, source):
        return pltpu.make_async_remote_copy(
            src_ref=terms_buf.at[c, k],
            dst_ref=gather_buf.at[c, source],
            send_sem=send1.at[c, k],
            recv_sem=recv1.at[c, source],
            device_id=(dest, me),
            device_id_type=MESH,
        )

    def decay_copy(k, dest, source):
        return pltpu.make_async_remote_copy(
            src_ref=dec_ref.at[:, pl.ds(k * LANE, LANE)],
            dst_ref=decay_buf.at[source],
            send_sem=send_d.at[k],
            recv_sem=recv_d.at[source],
            device_id=(dest, me),
            device_id_type=MESH,
        )

    def state_copy(c, dest, other, k):
        return pltpu.make_async_remote_copy(
            src_ref=chain_buf.at[c, dest],
            dst_ref=state_buf.at[c, k],
            send_sem=send2.at[c, dest],
            recv_sem=recv2.at[c, k],
            device_id=(other, me),
            device_id_type=MESH,
        )

    def sends_to(dest):
        return jnp.logical_and(n != dest, n < cuts - 1)

    def chain_send(c, terms):
        for k in range(cols):
            terms_buf[c, k] = terms[:, k * LANE : (k + 1) * LANE]
        for k in range(cols):

            @pl.when(sends_to(base + k))
            def _():
                term_copy(c, k, base + k, n).start()
                if c == 0:
                    decay_copy(k, base + k, n).start()

    def chain_turn(c):
        @pl.when(owner)
        def _():
            if c == 0:
                decay_buf[n] = dec_ref[:, pl.ds(lane, LANE)]
            gather_buf[c, n] = terms_buf[c, piece]
            state = init_ref[:, pl.ds(lane, LANE)]
            for s in range(cuts):
                chain_buf[c, s] = state

                @pl.when(n != s)
                def _():
                    state_copy(c, s, s, piece).start()
                    if s < cuts - 1:
                        term_copy(c, 0, s, s).wait_recv()
                        if c == 0:
                            decay_copy(0, s, s).wait_recv()

                if s < cuts - 1:
                    state = decay_buf[s] * state + gather_buf[c, s]
            state_buf[c, piece] = chain_buf[c, n]

    def chain_end(c):
        for k in range(cols):

            @pl.when(n != base + k)
            def _():
                state_copy(c, 0, base + k, k).wait_recv()

        return jnp.concatenate([state_buf[c, k] for k in range(cols)], axis=1)

    def drain(c):
        for k in range(cols):

            @pl.when(sends_to(base + k))
            def _():
                term_copy(c, k, base + k, n).wait_send()
                if c == 0:
                    decay_copy(k, base + k, n).wait_send()

        @pl.when(owner)
        def _():
            @pl.loop(1, cuts)
            def _(k):
                d = cut(k)
                state_copy(c, d, d, piece).wait_send()

    def current_copy(e, height, k, source):
        return pltpu.make_async_remote_copy(
            src_ref=part_buf.at[e, peer(k), pl.ds(0, height)],
            dst_ref=inflow_buf.at[e, source, pl.ds(0, height)],
            send_sem=send_x.at[e, k - 1],
            recv_sem=recv_x.at[e, source],
            device_id=(n, peer(k)),
            device_id_type=MESH,
        )

    def exchange_start(e, partial):
        height = partial.shape[0]
        for g in range(circ):
            part_buf[e, g, 0:height] = partial[:, g * ports : (g + 1) * ports]
        for k in range(1, circ):
            current_copy(e, height, k, me).start()

    def exchange_end(e, height):
        total = part_buf[e, me, 0:height]
        for k in range(1, circ):
            current_copy(e, height, k, peer(k)).wait_recv()
            total = total + inflow_buf[e, peer(k), 0:height]
        return total

    def exchange_drain(e, height):
        for k in range(1, circ):
            current_copy(e, height, k, me).wait_send()

    wide = min(256, nodes)

    def product(out, left, right):
        @pl.loop(0, nodes, step=wide)
        def _(at):
            at = pl.multiple_of(at, wide)
            out[:, pl.ds(at, wide)] = dot(left[...], right[:, pl.ds(at, wide)]).astype(BF16)

    for copy in loads[:4]:
        copy.wait()
    factor = jnp.broadcast_to(mem_ref[...], (LANE, nodes)).T
    for c in range(cols):
        at = slice(c * LANE, (c + 1) * LANE)
        turned = inv_ref[at, :].T
        inv_t[:, at] = turned
        pow1[:, at] = (turned.astype(F32) * factor).astype(BF16)
    for copy in loads[4:]:
        copy.wait()
    for g in range(circ):
        summed = jnp.zeros((ports, nodes), F32)
        for b in range(blocks):
            share = jnp.where(tgt_ref[0, b] == g, 1.0, 0.0).astype(F32)
            summed = summed + share * cw_ref[b].astype(F32)
        port_t[:, g * ports : (g + 1) * ports] = summed.astype(BF16).T

    load = src_ref[0:scen].astype(F32)
    for t in range(1, steps):
        load = load + src_ref[t * scen : (t + 1) * scen].astype(F32)
    pl.semaphore_wait(barrier, cuts - 1 + circ - 1)
    chain_send(0, load * (1.0 / steps))

    def one_step(values):
        exact = mem_ref[...] * values
        high = exact.astype(BF16)
        low = (exact - high.astype(F32)).astype(BF16)
        both = dot(jnp.concatenate([high, low], axis=0), inv_t[...])
        return both[: values.shape[0]] + both[values.shape[0] :]

    product(pow2, pow1, pow1)
    own[...] = dot(src_ref[...], inv_t[...])

    chain_turn(0)

    own[scen:] = own[scen:] + one_step(own[: rows - scen])
    product(pow4, pow2, pow2)
    span = 2
    for power in (pow2, pow4):
        if span < steps:
            own[span * scen :] = own[span * scen :] + dot(own[: rows - span * scen], power[...])
        span *= 2
    resp[0:ports] = inv_t[0:ports]
    resp[ports : 2 * ports] = dot(resp[0:ports], pow1[...]).astype(BF16)
    resp[2 * ports : 4 * ports] = dot(resp[0 : 2 * ports], pow2[...]).astype(BF16)
    resp[4 * ports : 8 * ports] = dot(resp[0 : 4 * ports], pow4[...]).astype(BF16)
    port_resp[...] = dot(resp[...], port_t[...]).astype(BF16)

    def by_lag(currents):
        low = currents.astype(BF16)
        columns = [low]
        for lag in range(1, steps):
            columns.append(
                jnp.concatenate(
                    [jnp.zeros((lag * scen, ports), BF16), low[: rows - lag * scen]], axis=0
                )
            )
        return jnp.concatenate(columns, axis=1)

    begin = chain_end(0)
    last = rows - scen
    for iteration in range(ITERS):
        first = iteration * SWEEPS
        exchange_start(first, dot(begin, port_t[...]))
        v0 = begin.astype(BF16)
        v1 = one_step(begin)
        v01 = jnp.concatenate([v0, v1.astype(BF16)], axis=0)
        v23 = dot(v01, pow2[...])
        v03 = jnp.concatenate([v01, v23.astype(BF16)], axis=0)
        v47 = dot(v03, pow4[...])
        v8 = dot(v47[0:scen], pow4[...])
        free[0:scen] = own[0:scen] + v1
        free[scen : 3 * scen] = own[scen : 3 * scen] + v23
        free[3 * scen : last] = own[3 * scen : last] + v47
        free[last:] = own[last:] + v8
        seen = dot(free[...], port_t[...])
        current = exchange_end(first, scen)
        current = jnp.concatenate([current] * steps, axis=0)
        for sweep in range(1, SWEEPS):
            exchange_start(first + sweep, seen + dot(by_lag(current), port_resp[...]))
            current = exchange_end(first + sweep, rows)
        lags = by_lag(current)
        if iteration < ITERS - 1:
            final = free[last:] + dot(lags[last:], resp[...])
        else:
            wave = free[...] + dot(lags, resp[...])
            wave_ref[...] = wave.astype(BF16)
            result = pltpu.make_async_copy(wave_ref, wave_out, sem_out)
            result.start()
            final = wave[last:]
        chain_send(iteration + 1, final - dec_ref[...] * begin)
        chain_turn(iteration + 1)
        begin = chain_end(iteration + 1)
    start_ref[...] = begin
    result.wait()

    for c in range(ITERS + 1):
        drain(c)
    for e in range(SWEEPS * ITERS):
        exchange_drain(e, scen if e % SWEEPS == 0 else rows)


def hand_over(start_in, wave_in, start_out, wave_out):
    start_out[...] = start_in[...]
    wave_out[...] = wave_in[...]


def solution(mesh):
    cuts, circ = mesh.shape["cuts"], mesh.shape["circ"]

    def shards(sources, inverse, memory, target, weight, decay, initial):
        steps, scen, nodes = sources.shape[1], sources.shape[3], sources.shape[4]
        blocks, ports = weight.shape[1], weight.shape[2]
        rows = steps * scen
        cols = nodes // LANE
        chains, swaps = ITERS + 1, ITERS * SWEEPS
        vmem = pl.BlockSpec(memory_space=pltpu.VMEM)
        hbm = pl.BlockSpec(memory_space=pl.ANY)
        dma = pltpu.SemaphoreType.DMA
        square = pltpu.VMEM((nodes, nodes), BF16)
        start, wave = pl.pallas_call(
            functools.partial(kernel, cuts, circ, steps),
            out_shape=(
                jax.ShapeDtypeStruct((scen, nodes), F32),
                jax.ShapeDtypeStruct((rows, nodes), BF16),
            ),
            in_specs=[hbm] * 7,
            out_specs=(vmem, hbm),
            scratch_shapes=[
                pltpu.VMEM((rows, nodes), BF16),
                square,
                pltpu.VMEM((1, nodes), F32),
                pltpu.SMEM((1, blocks), jnp.int32),
                pltpu.VMEM((blocks, ports, nodes), BF16),
                pltpu.VMEM((1, nodes), F32),
                pltpu.VMEM((scen, nodes), F32),
                pltpu.VMEM((rows, nodes), BF16),
                dma((7,)),
                dma(()),
                square,
                square,
                square,
                square,
                pltpu.VMEM((nodes, circ * ports), BF16),
                pltpu.VMEM((steps * ports, nodes), BF16),
                pltpu.VMEM((steps * ports, circ * ports), BF16),
                pltpu.VMEM((rows, nodes), F32),
                pltpu.VMEM((rows, nodes), F32),
                pltpu.VMEM((chains, cols, scen, LANE), F32),
                pltpu.VMEM((chains, cuts, scen, LANE), F32),
                pltpu.VMEM((chains, cuts, scen, LANE), F32),
                pltpu.VMEM((chains, cols, scen, LANE), F32),
                pltpu.VMEM((cuts, 1, LANE), F32),
                pltpu.VMEM((swaps, circ, rows, ports), F32),
                pltpu.VMEM((swaps, circ, rows, ports), F32),
                dma((chains, cols)),
                dma((chains, cuts)),
                dma((chains, cuts)),
                dma((chains, cols)),
                dma((cols,)),
                dma((cuts,)),
                dma((swaps, max(circ - 1, 1))),
                dma((swaps, circ)),
            ],
            compiler_params=pltpu.CompilerParams(
                collective_id=0, has_side_effects=True, vmem_limit_bytes=60 * 1024 * 1024
            ),
            name="parareal",
        )(
            sources.reshape(rows, nodes),
            inverse[0],
            memory.reshape(1, nodes),
            target,
            weight[0],
            decay.reshape(1, nodes),
            initial[0],
        )
        start, wave = pl.pallas_call(
            hand_over,
            out_shape=(
                jax.ShapeDtypeStruct(start.shape, F32),
                jax.ShapeDtypeStruct(wave.shape, BF16),
            ),
            in_specs=[vmem, vmem],
            out_specs=(vmem, vmem),
            name="hand_over",
        )(start, wave)
        return start[None, None], wave.reshape(1, steps, 1, scen, nodes)

    return jax.shard_map(
        shards,
        mesh=mesh,
        in_specs=(
            P("cuts", None, "circ", None, None),
            P("circ", None, None),
            P("cuts", "circ", None),
            P("circ", None),
            P("circ", None, None, None),
            P("cuts", "circ", None),
            P("circ", None, None),
        ),
        out_specs=(P("cuts", "circ", None, None), P("cuts", None, "circ", None, None)),
        check_vma=False,
    )
```

profile of v0, /device:TPU:8, one launch (start us, length us, event | category | flops | bytes accessed | tf_op | source)
XLA Modules:
  0.0 47.1 jit_solution(8651123869191276798)
XLA Ops:
  0.6 44.7 %parareal.1 = (f32[16,1024]{1,0:T(8,128)}, bf16[128,1024]{1,0:T(8,128)(2,1)}) custom-call(bf16[128,1024]{1,0:T(8,128)(2,1)} %bitcast.12, bf16[1024,1024]{1,0:T(8,128)(2,1)} %bitcast.10, f32[1,1024]{1,0:T(1,128)} %bitcast.14, s32[1,4]{1,0:T(1,128)} %tgt_in.1, bf16[4,128,1024]{2,1,0:T(8,128)(2,1)} %bitcast.11, f32[1,1024]{1,0:T(1,128)} %bitcast.15, ...), custom_call_target="tpu_custom_call" | custom-call | tf_op jit(solution)/shard_map/parareal/pallas_call | solution.py:357
  45.3 1.7 %hand_over.1 = (f32[16,1024]{1,0:T(8,128)}, bf16[128,1024]{1,0:T(8,128)(2,1)}) custom-call(f32[16,1024]{1,0:T(8,128)} %get-tuple-element.6.start_in, bf16[128,1024]{1,0:T(8,128)(2,1)} %get-tuple-element.7.wave_in), custom_call_target="tpu_custom_call" | custom-call | tf_op jit(solution)/shard_map/hand_over/pallas_call | solution.py:414
where the time goes:
time: 47.3 us; the launch traced here: 47.1 us
  Pallas kernels  46.4 us (98%)
  between operations  0.64 us (1%)
    pallas_call x1, Pallas kernels, shards(): pl.pallas_call(functools.partial(kernel, cuts, circ, steps), out_shape=(j...  44.7 us
    pallas_call x1, Pallas kernels, shards(): pl.pallas_call(hand_over, out_shape=(jax.ShapeDtypeStruct(start.shape, F3...  1.72 us

commit v1 on v0

--- a/solution.py
+++ b/solution.py
@@ -23,6 +23,7 @@
     cuts,
     circ,
     steps,
+    fused,
     src_in,
     inv_in,
     mem_in,
@@ -41,6 +42,7 @@
     init_ref,
     wave_ref,
     sem_in,
+    sem_inv,
     sem_out,
     inv_t,
     pow1,
@@ -48,7 +50,9 @@
     pow4,
     port_t,
     resp,
-    port_resp,
+    k_all,
+    k_sum,
+    k_me,
     own,
     free,
     terms_buf,
@@ -56,6 +60,8 @@
     chain_buf,
     state_buf,
     decay_buf,
+    u_buf,
+    y_buf,
     part_buf,
     inflow_buf,
     send1,
@@ -64,9 +70,16 @@
     recv2,
     send_d,
     recv_d,
+    send_k,
+    recv_k,
+    send_u,
+    recv_u,
+    send_y,
+    recv_y,
     send_x,
     recv_x,
 ):
+    scope = jax.named_scope
     n = lax.axis_index("cuts")
     me = lax.axis_index("circ")
     nodes = inv_ref.shape[0]
@@ -78,6 +91,8 @@
     piece = n - base
     owner = jnp.logical_and(n >= base, n < base + cols)
     lane = pl.multiple_of(piece * LANE, LANE)
+    mine = pl.ds(pl.multiple_of(me * ports, ports), ports)
+    last = rows - scen
 
     def cut(k):
         return lax.rem(n + k, cuts)
@@ -94,17 +109,21 @@
     for k in range(1, circ):
         pl.semaphore_signal(barrier, inc=1, device_id=(n, peer(k)), device_id_type=MESH)
 
-    pairs = (
-        (dec_in, dec_ref),
-        (src_in, src_ref),
-        (inv_in, inv_ref),
-        (mem_in, mem_ref),
-        (cw_in, cw_ref),
-        (tgt_in, tgt_ref),
-        (init_in, init_ref),
-    )
-    loads = [pltpu.make_async_copy(a, b, sem_in.at[k]) for k, (a, b) in enumerate(pairs)]
-    for copy in loads:
+    def load(k, a, b):
+        return pltpu.make_async_copy(a, b, sem_in.at[k])
+
+    first_loads = [load(0, src_in, src_ref), load(1, mem_in, mem_ref)]
+    last_loads = [
+        load(2, dec_in, dec_ref),
+        load(3, tgt_in, tgt_ref),
+        load(4, cw_in, cw_ref),
+        load(5, init_in, init_ref),
+    ]
+    strips = []
+    for c in range(cols):
+        at = pl.ds(c * LANE, LANE)
+        strips.append(pltpu.make_async_copy(inv_in.at[at], inv_ref.at[at], sem_inv.at[c]))
+    for copy in first_loads + strips + last_loads:
         copy.start()
 
     def term_copy(c, k, dest, source):
@@ -198,6 +217,32 @@
                 d = cut(k)
                 state_copy(c, d, d, piece).wait_send()
 
+    def swap_copy(ref, send, recv, k, source):
+        return pltpu.make_async_remote_copy(
+            src_ref=ref.at[me],
+            dst_ref=ref.at[source],
+            send_sem=send.at[k - 1],
+            recv_sem=recv.at[source],
+            device_id=(n, peer(k)),
+            device_id_type=MESH,
+        )
+
+    class Swap:
+        def __init__(self, *refs):
+            self.refs = refs
+
+        def start(self):
+            for k in range(1, circ):
+                swap_copy(*self.refs, k, me).start()
+
+        def wait(self):
+            for k in range(1, circ):
+                swap_copy(*self.refs, k, peer(k)).wait_recv()
+
+        def drain(self):
+            for k in range(1, circ):
+                swap_copy(*self.refs, k, me).wait_send()
+
     def current_copy(e, height, k, source):
         return pltpu.make_async_remote_copy(
             src_ref=part_buf.at[e, peer(k), pl.ds(0, height)],
@@ -229,33 +274,39 @@
     wide = min(256, nodes)
 
     def product(out, left, right):
-        @pl.loop(0, nodes, step=wide)
-        def _(at):
-            at = pl.multiple_of(at, wide)
-            out[:, pl.ds(at, wide)] = dot(left[...], right[:, pl.ds(at, wide)]).astype(BF16)
-
-    for copy in loads[:4]:
-        copy.wait()
-    factor = jnp.broadcast_to(mem_ref[...], (LANE, nodes)).T
+        for at in range(0, nodes, wide):
+            out[:, at : at + wide] = dot(left[...], right[:, at : at + wide]).astype(BF16)
+
+    with scope("w_src"):
+        for copy in first_loads:
+            copy.wait()
+    with scope("mean"):
+        mean = src_ref[0:scen].astype(F32)
+        for t in range(1, steps):
+            mean = mean + src_ref[t * scen : (t + 1) * scen].astype(F32)
+        mean = mean * (1.0 / steps)
+        factor = jnp.broadcast_to(mem_ref[...], (LANE, nodes)).T
     for c in range(cols):
         at = slice(c * LANE, (c + 1) * LANE)
+        with scope("w_inv"):
+            strips[c].wait()
         turned = inv_ref[at, :].T
         inv_t[:, at] = turned
         pow1[:, at] = (turned.astype(F32) * factor).astype(BF16)
-    for copy in loads[4:]:
-        copy.wait()
-    for g in range(circ):
-        summed = jnp.zeros((ports, nodes), F32)
-        for b in range(blocks):
-            share = jnp.where(tgt_ref[0, b] == g, 1.0, 0.0).astype(F32)
-            summed = summed + share * cw_ref[b].astype(F32)
-        port_t[:, g * ports : (g + 1) * ports] = summed.astype(BF16).T
-
-    load = src_ref[0:scen].astype(F32)
-    for t in range(1, steps):
-        load = load + src_ref[t * scen : (t + 1) * scen].astype(F32)
-    pl.semaphore_wait(barrier, cuts - 1 + circ - 1)
-    chain_send(0, load * (1.0 / steps))
+    with scope("w_rest"):
+        for copy in last_loads:
+            copy.wait()
+    with scope("w_barrier"):
+        pl.semaphore_wait(barrier, cuts - 1 + circ - 1)
+    chain_send(0, mean)
+
+    with scope("port_t"):
+        for g in range(circ):
+            summed = jnp.zeros((ports, nodes), F32)
+            for b in range(blocks):
+                share = jnp.where(tgt_ref[0, b] == g, 1.0, 0.0).astype(F32)
+                summed = summed + share * cw_ref[b].astype(F32)
+            port_t[:, g * ports : (g + 1) * ports] = summed.astype(BF16).T
 
     def one_step(values):
         exact = mem_ref[...] * values
@@ -264,26 +315,57 @@
         both = dot(jnp.concatenate([high, low], axis=0), inv_t[...])
         return both[: values.shape[0]] + both[values.shape[0] :]
 
-    product(pow2, pow1, pow1)
-    own[...] = dot(src_ref[...], inv_t[...])
-
-    chain_turn(0)
-
-    own[scen:] = own[scen:] + one_step(own[: rows - scen])
-    product(pow4, pow2, pow2)
-    span = 2
-    for power in (pow2, pow4):
-        if span < steps:
-            own[span * scen :] = own[span * scen :] + dot(own[: rows - span * scen], power[...])
-        span *= 2
-    resp[0:ports] = inv_t[0:ports]
-    resp[ports : 2 * ports] = dot(resp[0:ports], pow1[...]).astype(BF16)
-    resp[2 * ports : 4 * ports] = dot(resp[0 : 2 * ports], pow2[...]).astype(BF16)
-    resp[4 * ports : 8 * ports] = dot(resp[0 : 4 * ports], pow4[...]).astype(BF16)
-    port_resp[...] = dot(resp[...], port_t[...]).astype(BF16)
-
-    def by_lag(currents):
-        low = currents.astype(BF16)
+    with scope("pow2"):
+        product(pow2, pow1, pow1)
+    with scope("own0"):
+        own[...] = dot(src_ref[...], inv_t[...])
+        resp[0:ports] = inv_t[0:ports]
+
+    with scope("turn0"):
+        chain_turn(0)
+
+    with scope("own1"):
+        own[scen:] = own[scen:] + one_step(own[: rows - scen])
+        resp[ports : 2 * ports] = dot(resp[0:ports], pow1[...]).astype(BF16)
+
+    def beside(left, low, power):
+        count = left.shape[0]
+        both = dot(jnp.concatenate([left, resp[low * ports : (low + 2) * ports]], axis=0), power)
+        resp[(low + 2) * ports : (low + 4) * ports] = both[count:].astype(BF16)
+        return both[:count]
+
+    with scope("own2"):
+        own[2 * scen :] = own[2 * scen :] + beside(own[: rows - 2 * scen].astype(BF16), 0, pow2[...])
+    with scope("own4"):
+        ahead = beside(own[: rows - 4 * scen].astype(BF16), 2, pow2[...])
+        own[4 * scen :] = own[4 * scen :] + beside(ahead.astype(BF16), 4, pow2[...])
+
+    if fused:
+        k_swap = Swap(k_all, send_k, recv_k)
+        u_swaps = [Swap(u_buf.at[i], send_u.at[i], recv_u.at[i]) for i in range(ITERS)]
+        y_swaps = [Swap(y_buf.at[i], send_y.at[i], recv_y.at[i]) for i in range(ITERS)]
+
+        def take(j):
+            width = circ * ports
+            total = jnp.zeros((ports, width), F32)
+            for t in range(steps):
+                total = total + k_all[j, t * ports : (t + 1) * ports]
+                k_sum[pl.ds(pl.multiple_of(j * ports, ports), ports), t * width : (t + 1) * width] = (
+                    total.astype(BF16)
+                )
+            span = steps * ports
+            k_me[pl.ds(pl.multiple_of(j * span, span), span), :] = k_all[j, :, mine].astype(BF16)
+
+    with scope("port_resp"):
+        heard = dot(resp[...], port_t[...])
+        if fused:
+            k_all[me] = heard
+            k_swap.start()
+            take(me)
+        else:
+            k_me[...] = heard.astype(BF16)
+
+    def shifted(low):
         columns = [low]
         for lag in range(1, steps):
             columns.append(
@@ -291,49 +373,115 @@
                     [jnp.zeros((lag * scen, ports), BF16), low[: rows - lag * scen]], axis=0
                 )
             )
-        return jnp.concatenate(columns, axis=1)
-
-    begin = chain_end(0)
-    last = rows - scen
+        return columns
+
+    def by_lag(currents):
+        return jnp.concatenate(shifted(currents.astype(BF16)), axis=1)
+
+    def end_lags(currents):
+        low = currents.astype(BF16)
+        return jnp.concatenate(
+            [low[(steps - 1 - lag) * scen : (steps - lag) * scen] for lag in range(steps)], axis=1
+        )
+
+    with scope("end0"):
+        begin = chain_end(0)
     for iteration in range(ITERS):
         first = iteration * SWEEPS
-        exchange_start(first, dot(begin, port_t[...]))
-        v0 = begin.astype(BF16)
-        v1 = one_step(begin)
-        v01 = jnp.concatenate([v0, v1.astype(BF16)], axis=0)
-        v23 = dot(v01, pow2[...])
-        v03 = jnp.concatenate([v01, v23.astype(BF16)], axis=0)
-        v47 = dot(v03, pow4[...])
-        v8 = dot(v47[0:scen], pow4[...])
-        free[0:scen] = own[0:scen] + v1
-        free[scen : 3 * scen] = own[scen : 3 * scen] + v23
-        free[3 * scen : last] = own[3 * scen : last] + v47
-        free[last:] = own[last:] + v8
-        seen = dot(free[...], port_t[...])
-        current = exchange_end(first, scen)
-        current = jnp.concatenate([current] * steps, axis=0)
-        for sweep in range(1, SWEEPS):
-            exchange_start(first + sweep, seen + dot(by_lag(current), port_resp[...]))
-            current = exchange_end(first + sweep, rows)
-        lags = by_lag(current)
+        with scope("free"):
+            outflow = dot(begin, port_t[...])
+            if fused:
+                u_buf[iteration, me] = outflow
+                u_swaps[iteration].start()
+            else:
+                exchange_start(first, outflow)
+            v0 = begin.astype(BF16)
+            v1 = one_step(begin)
+            v2 = dot(v0, pow2[...])
+            v12 = jnp.concatenate([v1, v2], axis=0).astype(BF16)
+            v34 = dot(v12, pow2[...])
+            if iteration == 0:
+                v56 = dot(v34, pow2[...])
+                v78 = dot(v56, pow2[...])
+                v58 = jnp.concatenate([v56, v78], axis=0)
+            else:
+                v14 = jnp.concatenate([v12, v34.astype(BF16)], axis=0)
+                v58 = dot(v14, pow4[...])
+            free[0:scen] = own[0:scen] + v1
+            free[scen : 2 * scen] = own[scen : 2 * scen] + v2
+            free[2 * scen : 4 * scen] = own[2 * scen : 4 * scen] + v34
+            free[4 * scen :] = own[4 * scen :] + v58
+            seen = dot(free[...], port_t[...])
+        if fused:
+            with scope("y_start"):
+                y_buf[iteration, me] = seen
+                y_swaps[iteration].start()
+            with scope("w_k"):
+                if iteration == 0:
+                    k_swap.wait()
+                    for k in range(1, circ):
+                        take(peer(k))
+            with scope("w_u"):
+                u_swaps[iteration].wait()
+            with scope("ku"):
+                inflow = outflow
+                for k in range(1, circ):
+                    inflow = inflow + u_buf[iteration, peer(k)]
+                raised = dot(inflow, k_sum[...])
+                width = circ * ports
+                raised = jnp.concatenate(
+                    [raised[:, t * width : (t + 1) * width] for t in range(steps)], axis=0
+                )
+            with scope("w_y"):
+                y_swaps[iteration].wait()
+            with scope("sweep"):
+                total = seen
+                direct = y_buf[iteration, me, :, mine]
+                for k in range(1, circ):
+                    total = total + y_buf[iteration, peer(k)]
+                    direct = direct + y_buf[iteration, peer(k), :, mine]
+                second = (total + raised).astype(BF16)
+                columns = []
+                for g in range(circ):
+                    columns += shifted(second[:, g * ports : (g + 1) * ports])
+                current = direct + dot(jnp.concatenate(columns, axis=1), k_me[...])
+        else:
+            current = exchange_end(first, scen)
+            current = jnp.concatenate([current] * steps, axis=0)
+            for sweep in range(1, SWEEPS):
+                exchange_start(first + sweep, seen + dot(by_lag(current), k_me[...]))
+                current = exchange_end(first + sweep, rows)
+        with scope("final"):
+            final = free[last:] + dot(end_lags(current), resp[...])
+        with scope("send"):
+            chain_send(iteration + 1, final - dec_ref[...] * begin)
         if iteration < ITERS - 1:
-            final = free[last:] + dot(lags[last:], resp[...])
+            with scope("pow4"):
+                product(pow4, pow2, pow2)
         else:
-            wave = free[...] + dot(lags, resp[...])
-            wave_ref[...] = wave.astype(BF16)
-            result = pltpu.make_async_copy(wave_ref, wave_out, sem_out)
-            result.start()
-            final = wave[last:]
-        chain_send(iteration + 1, final - dec_ref[...] * begin)
-        chain_turn(iteration + 1)
-        begin = chain_end(iteration + 1)
-    start_ref[...] = begin
-    result.wait()
-
-    for c in range(ITERS + 1):
-        drain(c)
-    for e in range(SWEEPS * ITERS):
-        exchange_drain(e, scen if e % SWEEPS == 0 else rows)
+            with scope("wave"):
+                wave = free[...] + dot(by_lag(current), resp[...])
+                wave_ref[...] = wave.astype(BF16)
+                result = pltpu.make_async_copy(wave_ref, wave_out, sem_out)
+                result.start()
+        with scope("turn"):
+            chain_turn(iteration + 1)
+        with scope("end"):
+            begin = chain_end(iteration + 1)
+    with scope("out"):
+        start_ref[...] = begin
+        result.wait()
+
+    with scope("drain"):
+        for c in range(ITERS + 1):
+            drain(c)
+        if fused:
+            k_swap.drain()
+            for swap in u_swaps + y_swaps:
+                swap.drain()
+        else:
+            for e in range(SWEEPS * ITERS):
+                exchange_drain(e, scen if e % SWEEPS == 0 else rows)
 
 
 def hand_over(start_in, wave_in, start_out, wave_out):
@@ -350,12 +498,15 @@
         rows = steps * scen
         cols = nodes // LANE
         chains, swaps = ITERS + 1, ITERS * SWEEPS
+        others = max(circ - 1, 1)
+        fused = circ <= 2
+        span = steps * ports
         vmem = pl.BlockSpec(memory_space=pltpu.VMEM)
         hbm = pl.BlockSpec(memory_space=pl.ANY)
         dma = pltpu.SemaphoreType.DMA
         square = pltpu.VMEM((nodes, nodes), BF16)
         start, wave = pl.pallas_call(
-            functools.partial(kernel, cuts, circ, steps),
+            functools.partial(kernel, cuts, circ, steps, fused),
             out_shape=(
                 jax.ShapeDtypeStruct((scen, nodes), F32),
                 jax.ShapeDtypeStruct((rows, nodes), BF16),
@@ -371,7 +522,8 @@
                 pltpu.VMEM((1, nodes), F32),
                 pltpu.VMEM((scen, nodes), F32),
                 pltpu.VMEM((rows, nodes), BF16),
-                dma((7,)),
+                dma((6,)),
+                dma((cols,)),
                 dma(()),
                 square,
                 square,
@@ -379,7 +531,9 @@
                 square,
                 pltpu.VMEM((nodes, circ * ports), BF16),
                 pltpu.VMEM((steps * ports, nodes), BF16),
-                pltpu.VMEM((steps * ports, circ * ports), BF16),
+                pltpu.VMEM((circ if fused else 1, span if fused else 8, circ * ports), F32),
+                pltpu.VMEM((circ * ports, steps * circ * ports) if fused else (16, LANE), BF16),
+                pltpu.VMEM((circ * span, ports) if fused else (span, circ * ports), BF16),
                 pltpu.VMEM((rows, nodes), F32),
                 pltpu.VMEM((rows, nodes), F32),
                 pltpu.VMEM((chains, cols, scen, LANE), F32),
@@ -387,15 +541,23 @@
                 pltpu.VMEM((chains, cuts, scen, LANE), F32),
                 pltpu.VMEM((chains, cols, scen, LANE), F32),
                 pltpu.VMEM((cuts, 1, LANE), F32),
-                pltpu.VMEM((swaps, circ, rows, ports), F32),
-                pltpu.VMEM((swaps, circ, rows, ports), F32),
+                pltpu.VMEM((ITERS, circ, scen, circ * ports), F32),
+                pltpu.VMEM((ITERS, circ, rows, circ * ports), F32),
+                pltpu.VMEM((1, 1, 8, LANE) if fused else (swaps, circ, rows, ports), F32),
+                pltpu.VMEM((1, 1, 8, LANE) if fused else (swaps, circ, rows, ports), F32),
                 dma((chains, cols)),
                 dma((chains, cuts)),
                 dma((chains, cuts)),
                 dma((chains, cols)),
                 dma((cols,)),
                 dma((cuts,)),
-                dma((swaps, max(circ - 1, 1))),
+                dma((others,)),
+                dma((circ,)),
+                dma((ITERS, others)),
+                dma((ITERS, circ)),
+                dma((ITERS, others)),
+                dma((ITERS, circ)),
+                dma((swaps, others)),
                 dma((swaps, circ)),
             ],
             compiler_params=pltpu.CompilerParams(

time: 47.3 us -> 42.2 us (0.89)
  Pallas kernels: 46.4 us -> 41.4 us
    pallas_call x1, Pallas kernels: 44.7 us -> 39.7 us  [shards(): pl.pallas_call(functools.partial(kernel, cuts, circ, steps, fused), out_s...]
where the time goes in v1:
time: 42.2 us; the launch traced here: 42 us
  Pallas kernels  41.4 us (98%)
  between operations  0.64 us (2%)
    pallas_call x1, Pallas kernels, shards(): pl.pallas_call(functools.partial(kernel, cuts, circ, steps, fused), out_s...  39.7 us
    pallas_call x1, Pallas kernels, shards(): pl.pallas_call(hand_over, out_shape=(jax.ShapeDtypeStruct(start.shape, F3...  1.72 us

profile of v1, /device:TPU:8, one launch (start us, length us, event | category | flops | bytes accessed | tf_op | source)
XLA Modules:
  0.0 42.0 jit_solution(16495571933084485229)
XLA Ops:
  0.6 39.7 %parareal.1 = (f32[16,1024]{1,0:T(8,128)}, bf16[128,1024]{1,0:T(8,128)(2,1)}) custom-call(bf16[128,1024]{1,0:T(8,128)(2,1)} %bitcast.12, bf16[1024,1024]{1,0:T(8,128)(2,1)} %bitcast.10, f32[1,1024]{1,0:T(1,128)} %bitcast.14, s32[1,4]{1,0:T(1,128)} %tgt_in.1, bf16[4,128,1024]{2,1,0:T(8,128)(2,1)} %bitcast.11, f32[1,1024]{1,0:T(1,128)} %bitcast.15, ...), custom_call_target="tpu_custom_call" | custom-call | tf_op jit(solution)/shard_map/parareal/pallas_call | solution.py:508
  40.3 1.7 %hand_over.1 = (f32[16,1024]{1,0:T(8,128)}, bf16[128,1024]{1,0:T(8,128)(2,1)}) custom-call(f32[16,1024]{1,0:T(8,128)} %get-tuple-element.6.start_in, bf16[128,1024]{1,0:T(8,128)(2,1)} %get-tuple-element.7.wave_in), custom_call_target="tpu_custom_call" | custom-call | tf_op jit(solution)/shard_map/hand_over/pallas_call | solution.py:576

commit v2 on v1

--- a/solution.py
+++ b/solution.py
@@ -1,4 +1,5 @@
 import functools
+import math
 
 import jax
 import jax.numpy as jnp
@@ -32,7 +33,7 @@
     dec_in,
     init_in,
     start_ref,
-    wave_out,
+    wave_ref,
     src_ref,
     inv_ref,
     mem_ref,
@@ -40,26 +41,26 @@
     cw_ref,
     dec_ref,
     init_ref,
-    wave_ref,
     sem_in,
     sem_inv,
-    sem_out,
     inv_t,
     pow1,
     pow2,
     pow4,
-    port_t,
+    seen_t,
     resp,
     k_all,
     k_sum,
     k_me,
     own,
+    own_seen,
     free,
     terms_buf,
     gather_buf,
     chain_buf,
     state_buf,
     decay_buf,
+    origin_buf,
     u_buf,
     y_buf,
     part_buf,
@@ -70,6 +71,8 @@
     recv2,
     send_d,
     recv_d,
+    send_o,
+    recv_o,
     send_k,
     recv_k,
     send_u,
@@ -92,7 +95,14 @@
     owner = jnp.logical_and(n >= base, n < base + cols)
     lane = pl.multiple_of(piece * LANE, LANE)
     mine = pl.ds(pl.multiple_of(me * ports, ports), ports)
+    swapped = circ % 2 == 0
+    mate = me + 1 - 2 * lax.rem(me, 2) if swapped else me
+    plane = math.gcd(cuts, 4)
+    high = terms_buf.shape[2]
+    parts = scen // high
     last = rows - scen
+    width = circ * ports
+    port_t = seen_t.at[:, 0:width]
 
     def cut(k):
         return lax.rem(n + k, cuts)
@@ -102,9 +112,16 @@
 
     barrier = pltpu.get_barrier_semaphore()
 
-    @pl.loop(1, cuts)
-    def _(k):
-        pl.semaphore_signal(barrier, inc=1, device_id=(cut(k), me), device_id_type=MESH)
+    @pl.when(owner)
+    def _():
+        @pl.loop(1, cuts)
+        def _(k):
+            pl.semaphore_signal(barrier, inc=1, device_id=(cut(k), mate), device_id_type=MESH)
+
+    @pl.when(jnp.logical_not(owner))
+    def _():
+        for k in range(cols):
+            pl.semaphore_signal(barrier, inc=1, device_id=(base + k, mate), device_id_type=MESH)
 
     for k in range(1, circ):
         pl.semaphore_signal(barrier, inc=1, device_id=(n, peer(k)), device_id_type=MESH)
@@ -126,96 +143,171 @@
     for copy in first_loads + strips + last_loads:
         copy.start()
 
-    def term_copy(c, k, dest, source):
+    def term_copy(e, k, dest):
         return pltpu.make_async_remote_copy(
-            src_ref=terms_buf.at[c, k],
-            dst_ref=gather_buf.at[c, source],
-            send_sem=send1.at[c, k],
-            recv_sem=recv1.at[c, source],
-            device_id=(dest, me),
+            src_ref=terms_buf.at[e, k],
+            dst_ref=gather_buf.at[e, n],
+            send_sem=send1.at[e, k],
+            recv_sem=recv1.at[e, n // plane],
+            device_id=(dest, mate),
             device_id_type=MESH,
         )
 
-    def decay_copy(k, dest, source):
+    def decay_copy(k, dest):
         return pltpu.make_async_remote_copy(
             src_ref=dec_ref.at[:, pl.ds(k * LANE, LANE)],
-            dst_ref=decay_buf.at[source],
+            dst_ref=decay_buf.at[n],
             send_sem=send_d.at[k],
-            recv_sem=recv_d.at[source],
-            device_id=(dest, me),
+            recv_sem=recv_d,
+            device_id=(dest, mate),
             device_id_type=MESH,
         )
 
-    def state_copy(c, dest, other, k):
+    def origin_copy():
         return pltpu.make_async_remote_copy(
-            src_ref=chain_buf.at[c, dest],
-            dst_ref=state_buf.at[c, k],
-            send_sem=send2.at[c, dest],
-            recv_sem=recv2.at[c, k],
-            device_id=(other, me),
+            src_ref=init_ref.at[:, pl.ds(lane, LANE)],
+            dst_ref=origin_buf,
+            send_sem=send_o,
+            recv_sem=recv_o,
+            device_id=(n, mate),
             device_id_type=MESH,
         )
 
+    def state_copy(e, dest, k):
+        return pltpu.make_async_remote_copy(
+            src_ref=chain_buf.at[e, dest],
+            dst_ref=state_buf.at[e, k],
+            send_sem=send2.at[e, dest],
+            recv_sem=recv2.at[e, k],
+            device_id=(dest, mate),
+            device_id_type=MESH,
+        )
+
+    def landed(buffer, recv, count):
+        return pltpu.make_async_remote_copy(
+            src_ref=buffer.at[pl.ds(0, count)],
+            dst_ref=buffer.at[pl.ds(0, count)],
+            send_sem=send_o,
+            recv_sem=recv,
+            device_id=(n, mate),
+            device_id_type=MESH,
+        )
+
+    def apart(other):
+        return True if swapped else n != other
+
     def sends_to(dest):
-        return jnp.logical_and(n != dest, n < cuts - 1)
+        return n < cuts - 1 if swapped else jnp.logical_and(n != dest, n < cuts - 1)
 
     def chain_send(c, terms):
-        for k in range(cols):
-            terms_buf[c, k] = terms[:, k * LANE : (k + 1) * LANE]
-        for k in range(cols):
-
-            @pl.when(sends_to(base + k))
+        for h in range(parts):
+            for k in range(cols):
+                terms_buf[c * parts + h, k] = terms[
+                    h * high : (h + 1) * high, k * LANE : (k + 1) * LANE
+                ]
+
+        def push(order):
+            for e in range(c * parts, (c + 1) * parts):
+                for k in order:
+
+                    @pl.when(sends_to(base + k))
+                    def _():
+                        term_copy(e, k, base + k).start()
+
+        @pl.when(n < cuts // 2)
+        def _():
+            push(range(cols - 1, -1, -1))
+
+        @pl.when(n >= cuts // 2)
+        def _():
+            push(range(cols))
+
+    def wait_landed(buffer, recv, first, stop):
+        count = min(stop, cuts - 1) - first
+        if swapped:
+            landed(buffer, recv, count).wait_recv()
+        else:
+            here = jnp.logical_and(n >= first, n < first + count)
+
+            @pl.when(here)
             def _():
-                term_copy(c, k, base + k, n).start()
-                if c == 0:
-                    decay_copy(k, base + k, n).start()
+                if count > 1:
+                    landed(buffer, recv, count - 1).wait_recv()
+
+            @pl.when(jnp.logical_not(here))
+            def _():
+                landed(buffer, recv, count).wait_recv()
 
     def chain_turn(c):
         @pl.when(owner)
         def _():
             if c == 0:
-                decay_buf[n] = dec_ref[:, pl.ds(lane, LANE)]
-            gather_buf[c, n] = terms_buf[c, piece]
-            state = init_ref[:, pl.ds(lane, LANE)]
-            for s in range(cuts):
-                chain_buf[c, s] = state
-
-                @pl.when(n != s)
+                wait_landed(decay_buf, recv_d, 0, cuts)
+                if swapped:
+                    origin_copy().wait_recv()
+                else:
+                    decay_buf[n] = dec_ref[:, pl.ds(lane, LANE)]
+                    origin_buf[...] = init_ref[:, pl.ds(lane, LANE)]
+            for h in range(parts):
+                e = c * parts + h
+                if not swapped:
+                    gather_buf[e, n] = terms_buf[e, piece]
+                state = origin_buf[h * high : (h + 1) * high]
+                for s in range(cuts):
+                    chain_buf[e, s] = state
+                    if s > 0:
+
+                        @pl.when(apart(s))
+                        def _():
+                            state_copy(e, s, piece).start()
+
+                    if s < cuts - 1:
+                        if s % plane == 0:
+                            group = recv1.at[e, s // plane]
+                            wait_landed(gather_buf.at[e], group, s, s + plane)
+                        state = decay_buf[s] * state + gather_buf[e, s]
+                if not swapped:
+                    state_buf[e, piece] = chain_buf[e, n]
+
+    def chain_end(c):
+        blocks = range(c * parts, (c + 1) * parts)
+        for e in blocks:
+            for k in range(cols):
+
+                @pl.when(jnp.logical_and(apart(base + k), n > 0))
                 def _():
-                    state_copy(c, s, s, piece).start()
-                    if s < cuts - 1:
-                        term_copy(c, 0, s, s).wait_recv()
-                        if c == 0:
-                            decay_copy(0, s, s).wait_recv()
-
-                if s < cuts - 1:
-                    state = decay_buf[s] * state + gather_buf[c, s]
-            state_buf[c, piece] = chain_buf[c, n]
-
-    def chain_end(c):
-        for k in range(cols):
-
-            @pl.when(n != base + k)
-            def _():
-                state_copy(c, 0, base + k, k).wait_recv()
-
-        return jnp.concatenate([state_buf[c, k] for k in range(cols)], axis=1)
+                    state_copy(e, 0, k).wait_recv()
+
+        return jnp.concatenate(
+            [jnp.concatenate([state_buf[e, k] for k in range(cols)], axis=1) for e in blocks],
+            axis=0,
+        )
 
     def drain(c):
-        for k in range(cols):
-
-            @pl.when(sends_to(base + k))
-            def _():
-                term_copy(c, k, base + k, n).wait_send()
-                if c == 0:
-                    decay_copy(k, base + k, n).wait_send()
+        for e in range(c * parts, (c + 1) * parts):
+            for k in range(cols):
+
+                @pl.when(sends_to(base + k))
+                def _():
+                    term_copy(e, k, base + k).wait_send()
+
+        if c == 0:
+            for k in range(cols):
+
+                @pl.when(sends_to(base + k))
+                def _():
+                    decay_copy(k, base + k).wait_send()
 
         @pl.when(owner)
         def _():
-            @pl.loop(1, cuts)
-            def _(k):
-                d = cut(k)
-                state_copy(c, d, d, piece).wait_send()
+            if c == 0 and swapped:
+                origin_copy().wait_send()
+            for e in range(c * parts, (c + 1) * parts):
+                for s in range(1, cuts):
+
+                    @pl.when(apart(s))
+                    def _():
+                        state_copy(e, s, piece).wait_send()
 
     def swap_copy(ref, send, recv, k, source):
         return pltpu.make_async_remote_copy(
@@ -296,9 +388,36 @@
     with scope("w_rest"):
         for copy in last_loads:
             copy.wait()
+
+    @pl.when(n == 0)
+    def _():
+        for e in range((ITERS + 1) * parts):
+            top = e % parts * high
+            for k in range(cols):
+                state_buf[e, k] = init_ref[top : top + high, k * LANE : (k + 1) * LANE]
+
     with scope("w_barrier"):
-        pl.semaphore_wait(barrier, cuts - 1 + circ - 1)
+
+        @pl.when(owner)
+        def _():
+            pl.semaphore_wait(barrier, cuts - 1 + circ - 1)
+
+        @pl.when(jnp.logical_not(owner))
+        def _():
+            pl.semaphore_wait(barrier, cols + circ - 1)
+
     chain_send(0, mean)
+    for k in range(cols):
+
+        @pl.when(sends_to(base + k))
+        def _():
+            decay_copy(k, base + k).start()
+
+    if swapped:
+
+        @pl.when(owner)
+        def _():
+            origin_copy().start()
 
     with scope("port_t"):
         for g in range(circ):
@@ -321,12 +440,12 @@
         own[...] = dot(src_ref[...], inv_t[...])
         resp[0:ports] = inv_t[0:ports]
 
-    with scope("turn0"):
-        chain_turn(0)
-
     with scope("own1"):
         own[scen:] = own[scen:] + one_step(own[: rows - scen])
         resp[ports : 2 * ports] = dot(resp[0:ports], pow1[...]).astype(BF16)
+
+    with scope("turn0"):
+        chain_turn(0)
 
     def beside(left, low, power):
         count = left.shape[0]
@@ -346,7 +465,6 @@
         y_swaps = [Swap(y_buf.at[i], send_y.at[i], recv_y.at[i]) for i in range(ITERS)]
 
         def take(j):
-            width = circ * ports
             total = jnp.zeros((ports, width), F32)
             for t in range(steps):
                 total = total + k_all[j, t * ports : (t + 1) * ports]
@@ -361,7 +479,6 @@
         if fused:
             k_all[me] = heard
             k_swap.start()
-            take(me)
         else:
             k_me[...] = heard.astype(BF16)
 
@@ -384,43 +501,53 @@
             [low[(steps - 1 - lag) * scen : (steps - lag) * scen] for lag in range(steps)], axis=1
         )
 
+    def keep():
+        free[0:scen] = own[0:scen] + v1
+        free[scen : 2 * scen] = own[scen : 2 * scen] + v2
+        free[2 * scen : 4 * scen] = own[2 * scen : 4 * scen] + v34
+        free[4 * scen :] = own[4 * scen :] + v58
+
     with scope("end0"):
         begin = chain_end(0)
     for iteration in range(ITERS):
         first = iteration * SWEEPS
         with scope("free"):
-            outflow = dot(begin, port_t[...])
+            v0 = begin.astype(BF16)
+            outflow = dot(v0, port_t[...])
+            v1 = one_step(begin)
+            v2 = dot(v0, pow2[...])
+            v12 = jnp.concatenate([v1, v2], axis=0).astype(BF16)
             if fused:
                 u_buf[iteration, me] = outflow
                 u_swaps[iteration].start()
             else:
                 exchange_start(first, outflow)
-            v0 = begin.astype(BF16)
-            v1 = one_step(begin)
-            v2 = dot(v0, pow2[...])
-            v12 = jnp.concatenate([v1, v2], axis=0).astype(BF16)
-            v34 = dot(v12, pow2[...])
             if iteration == 0:
+                v34 = dot(v12, pow2[...])
                 v56 = dot(v34, pow2[...])
                 v78 = dot(v56, pow2[...])
                 v58 = jnp.concatenate([v56, v78], axis=0)
+                keep()
+                seen = dot(free[...], port_t[...])
             else:
-                v14 = jnp.concatenate([v12, v34.astype(BF16)], axis=0)
-                v58 = dot(v14, pow4[...])
-            free[0:scen] = own[0:scen] + v1
-            free[scen : 2 * scen] = own[scen : 2 * scen] + v2
-            free[2 * scen : 4 * scen] = own[2 * scen : 4 * scen] + v34
-            free[4 * scen :] = own[4 * scen :] + v58
-            seen = dot(free[...], port_t[...])
+                heard = dot(v12, seen_t[...])
+                pairs = [heard[:, k * width : (k + 1) * width] for k in range(steps // 2)]
+                seen = own_seen[...] + jnp.concatenate(pairs, axis=0)
         if fused:
             with scope("y_start"):
                 y_buf[iteration, me] = seen
                 y_swaps[iteration].start()
             with scope("w_k"):
                 if iteration == 0:
+                    take(me)
                     k_swap.wait()
                     for k in range(1, circ):
                         take(peer(k))
+            if iteration > 0:
+                with scope("later"):
+                    v34 = dot(v12, pow2[...])
+                    v58 = dot(jnp.concatenate([v12, v34.astype(BF16)], axis=0), pow4[...])
+                    free[last:] = own[last:] + v58[3 * scen :]
             with scope("w_u"):
                 u_swaps[iteration].wait()
             with scope("ku"):
@@ -428,7 +555,6 @@
                 for k in range(1, circ):
                     inflow = inflow + u_buf[iteration, peer(k)]
                 raised = dot(inflow, k_sum[...])
-                width = circ * ports
                 raised = jnp.concatenate(
                     [raised[:, t * width : (t + 1) * width] for t in range(steps)], axis=0
                 )
@@ -446,6 +572,10 @@
                     columns += shifted(second[:, g * ports : (g + 1) * ports])
                 current = direct + dot(jnp.concatenate(columns, axis=1), k_me[...])
         else:
+            if iteration > 0:
+                v34 = dot(v12, pow2[...])
+                v58 = dot(jnp.concatenate([v12, v34.astype(BF16)], axis=0), pow4[...])
+                free[last:] = own[last:] + v58[3 * scen :]
             current = exchange_end(first, scen)
             current = jnp.concatenate([current] * steps, axis=0)
             for sweep in range(1, SWEEPS):
@@ -458,19 +588,23 @@
         if iteration < ITERS - 1:
             with scope("pow4"):
                 product(pow4, pow2, pow2)
+                seen_t[:, width : 2 * width] = dot(pow2[...], port_t[...]).astype(BF16)
+                own_seen[...] = dot(own[...], port_t[...])
         else:
             with scope("wave"):
+                keep()
                 wave = free[...] + dot(by_lag(current), resp[...])
                 wave_ref[...] = wave.astype(BF16)
-                result = pltpu.make_async_copy(wave_ref, wave_out, sem_out)
-                result.start()
         with scope("turn"):
             chain_turn(iteration + 1)
+        if iteration < ITERS - 1:
+            with scope("seen_t"):
+                half = seen_t[:, 0 : 2 * width]
+                seen_t[:, 2 * width : 4 * width] = dot(pow4[...], half).astype(BF16)
         with scope("end"):
             begin = chain_end(iteration + 1)
     with scope("out"):
         start_ref[...] = begin
-        result.wait()
 
     with scope("drain"):
         for c in range(ITERS + 1):
@@ -484,9 +618,15 @@
                 exchange_drain(e, scen if e % SWEEPS == 0 else rows)
 
 
-def hand_over(start_in, wave_in, start_out, wave_out):
-    start_out[...] = start_in[...]
-    wave_out[...] = wave_in[...]
+def hand_over(start_in, wave_in, start_out, wave_out, sems):
+    copies = [
+        pltpu.make_async_copy(start_in, start_out, sems.at[0]),
+        pltpu.make_async_copy(wave_in, wave_out, sems.at[1]),
+    ]
+    for copy in copies:
+        copy.start()
+    for copy in copies:
+        copy.wait()
 
 
 def solution(mesh):
@@ -497,7 +637,8 @@
         blocks, ports = weight.shape[1], weight.shape[2]
         rows = steps * scen
         cols = nodes // LANE
-        chains, swaps = ITERS + 1, ITERS * SWEEPS
+        high = scen
+        chains, swaps = (ITERS + 1) * (scen // high), ITERS * SWEEPS
         others = max(circ - 1, 1)
         fused = circ <= 2
         span = steps * ports
@@ -507,12 +648,9 @@
         square = pltpu.VMEM((nodes, nodes), BF16)
         start, wave = pl.pallas_call(
             functools.partial(kernel, cuts, circ, steps, fused),
-            out_shape=(
-                jax.ShapeDtypeStruct((scen, nodes), F32),
-                jax.ShapeDtypeStruct((rows, nodes), BF16),
-            ),
+            out_shape=(pltpu.VMEM((scen, nodes), F32), pltpu.VMEM((rows, nodes), BF16)),
             in_specs=[hbm] * 7,
-            out_specs=(vmem, hbm),
+            out_specs=(vmem, vmem),
             scratch_shapes=[
                 pltpu.VMEM((rows, nodes), BF16),
                 square,
@@ -521,26 +659,26 @@
                 pltpu.VMEM((blocks, ports, nodes), BF16),
                 pltpu.VMEM((1, nodes), F32),
                 pltpu.VMEM((scen, nodes), F32),
-                pltpu.VMEM((rows, nodes), BF16),
                 dma((6,)),
                 dma((cols,)),
-                dma(()),
                 square,
                 square,
                 square,
                 square,
-                pltpu.VMEM((nodes, circ * ports), BF16),
+                pltpu.VMEM((nodes, steps // 2 * circ * ports), BF16),
                 pltpu.VMEM((steps * ports, nodes), BF16),
                 pltpu.VMEM((circ if fused else 1, span if fused else 8, circ * ports), F32),
                 pltpu.VMEM((circ * ports, steps * circ * ports) if fused else (16, LANE), BF16),
                 pltpu.VMEM((circ * span, ports) if fused else (span, circ * ports), BF16),
                 pltpu.VMEM((rows, nodes), F32),
+                pltpu.VMEM((rows, circ * ports), F32),
                 pltpu.VMEM((rows, nodes), F32),
-                pltpu.VMEM((chains, cols, scen, LANE), F32),
-                pltpu.VMEM((chains, cuts, scen, LANE), F32),
-                pltpu.VMEM((chains, cuts, scen, LANE), F32),
-                pltpu.VMEM((chains, cols, scen, LANE), F32),
+                pltpu.VMEM((chains, cols, high, LANE), F32),
+                pltpu.VMEM((chains, cuts, high, LANE), F32),
+                pltpu.VMEM((chains, cuts, high, LANE), F32),
+                pltpu.VMEM((chains, cols, high, LANE), F32),
                 pltpu.VMEM((cuts, 1, LANE), F32),
+                pltpu.VMEM((scen, LANE), F32),
                 pltpu.VMEM((ITERS, circ, scen, circ * ports), F32),
                 pltpu.VMEM((ITERS, circ, rows, circ * ports), F32),
                 pltpu.VMEM((1, 1, 8, LANE) if fused else (swaps, circ, rows, ports), F32),
@@ -550,7 +688,9 @@
                 dma((chains, cuts)),
                 dma((chains, cols)),
                 dma((cols,)),
-                dma((cuts,)),
+                dma(()),
+                dma(()),
+                dma(()),
                 dma((others,)),
                 dma((circ,)),
                 dma((ITERS, others)),
@@ -573,6 +713,7 @@
             decay.reshape(1, nodes),
             initial[0],
         )
+        start, wave = (pltpu.with_memory_space_constraint(x, pltpu.VMEM) for x in (start, wave))
         start, wave = pl.pallas_call(
             hand_over,
             out_shape=(
@@ -580,7 +721,8 @@
                 jax.ShapeDtypeStruct(wave.shape, BF16),
             ),
             in_specs=[vmem, vmem],
-            out_specs=(vmem, vmem),
+            out_specs=(hbm, hbm),
+            scratch_shapes=[dma((2,))],
             name="hand_over",
         )(start, wave)
         return start[None, None], wave.reshape(1, steps, 1, scen, nodes)

time: 42.2 us -> 40 us (0.948)
  the two profiles are of different devices: /device:TPU:8 before, /device:TPU:5 now
where the time goes in v2:
time: 40 us; the launch traced here: 39.8 us
  Pallas kernels  39 us (98%)
  between operations  0.8 us (2%)
    pallas_call x1, Pallas kernels, shards(): pl.pallas_call(functools.partial(kernel, cuts, circ, steps, fused), out_s...  38.3 us

profile of v2, /device:TPU:5, one launch (start us, length us, event | category | flops | bytes accessed | tf_op | source)
XLA Modules:
  0.0 39.8 jit_solution(12511385844677379687)
XLA Ops:
  0.6 38.3 %parareal.1 = (f32[16,1024]{1,0:T(8,128)S(1)}, bf16[128,1024]{1,0:T(8,128)(2,1)S(1)}) custom-call(bf16[128,1024]{1,0:T(8,128)(2,1)} %bitcast.12, bf16[1024,1024]{1,0:T(8,128)(2,1)} %bitcast.10, f32[1,1024]{1,0:T(1,128)} %bitcast.14, s32[1,4]{1,0:T(1,128)} %tgt_in.1, bf16[4,128,1024]{2,1,0:T(8,128)(2,1)} %bitcast.11, f32[1,1024]{1,0:T(1,128)} %bitcast.15, ...), custom_call_target="tpu_custom_call" | custom-call | tf_op jit(solution)/shard_map/parareal/pallas_call | solution.py:649
  38.9 0.7 %hand_over.1 = (f32[16,1024]{1,0:T(8,128)}, bf16[128,1024]{1,0:T(8,128)(2,1)}) custom-call(f32[16,1024]{1,0:T(8,128)S(1)} %get-tuple-element.6.start_in, bf16[128,1024]{1,0:T(8,128)(2,1)S(1)} %get-tuple-element.7.wave_in), custom_call_target="tpu_custom_call" | custom-call | tf_op jit(solution)/shard_map/hand_over/pallas_call | solution.py:717

commit v3 on v2

--- a/solution.py
+++ b/solution.py
@@ -61,6 +61,12 @@
     state_buf,
     decay_buf,
     origin_buf,
+    near_buf,
+    near_chain,
+    near_dec,
+    near_prod,
+    side_buf,
+    scale_buf,
     u_buf,
     y_buf,
     part_buf,
@@ -73,6 +79,14 @@
     recv_d,
     send_o,
     recv_o,
+    send_n1,
+    recv_n1,
+    send_n2,
+    recv_n2,
+    send_nd,
+    recv_nd,
+    send_np,
+    recv_np,
     send_k,
     recv_k,
     send_u,
@@ -104,6 +118,15 @@
     width = circ * ports
     port_t = seen_t.at[:, 0:width]
 
+    near = swapped and 1 < plane <= base and cols % plane == 0
+    per = cols // plane
+    tail = cuts - plane if near else cuts - 1
+    edge = jnp.logical_or(n < plane, n >= cuts - plane)
+    rim = jnp.where(n < plane, 0, cuts - plane)
+    rank = n - rim
+    behind = jnp.logical_and(edge, rank > 0)
+    ahead_of = jnp.logical_and(edge, rank < plane - 1)
+
     def cut(k):
         return lax.rem(n + k, cuts)
 
@@ -122,6 +145,14 @@
     def _():
         for k in range(cols):
             pl.semaphore_signal(barrier, inc=1, device_id=(base + k, mate), device_id_type=MESH)
+
+    if near:
+
+        @pl.when(edge)
+        def _():
+            for k in range(1, plane):
+                other = rim + lax.rem(rank + k, plane)
+                pl.semaphore_signal(barrier, inc=1, device_id=(other, mate), device_id_type=MESH)
 
     for k in range(1, circ):
         pl.semaphore_signal(barrier, inc=1, device_id=(n, peer(k)), device_id_type=MESH)
@@ -173,6 +204,104 @@
             device_id_type=MESH,
         )
 
+    def near_term(c, q):
+        return pltpu.make_async_remote_copy(
+            src_ref=terms_buf.at[c, pl.ds(q * per, per)],
+            dst_ref=near_buf.at[c, rank],
+            send_sem=send_n1.at[c, q],
+            recv_sem=recv_n1.at[c],
+            device_id=(rim + q, mate),
+            device_id_type=MESH,
+        )
+
+    def near_decay(q):
+        return pltpu.make_async_remote_copy(
+            src_ref=dec_ref.at[:, pl.ds(q * per * LANE, per * LANE)],
+            dst_ref=near_dec.at[rank],
+            send_sem=send_nd.at[q],
+            recv_sem=recv_nd,
+            device_id=(rim + q, mate),
+            device_id_type=MESH,
+        )
+
+    def near_scale(t, q):
+        return pltpu.make_async_remote_copy(
+            src_ref=near_prod.at[t],
+            dst_ref=scale_buf.at[:, pl.ds(q * per * LANE, per * LANE)],
+            send_sem=send_np.at[t],
+            recv_sem=recv_np.at[q],
+            device_id=(rim + t, mate),
+            device_id_type=MESH,
+        )
+
+    def near_state(c, t, q):
+        return pltpu.make_async_remote_copy(
+            src_ref=near_chain.at[c, t],
+            dst_ref=side_buf.at[c, pl.ds(q * per, per)],
+            send_sem=send_n2.at[c, t],
+            recv_sem=recv_n2.at[c, q],
+            device_id=(rim + t, mate),
+            device_id_type=MESH,
+        )
+
+    def near_send(c):
+        if near:
+
+            @pl.when(ahead_of)
+            def _():
+                for q in range(plane):
+                    near_term(c, q).start()
+                    if c == 0:
+                        near_decay(q).start()
+
+    def near_turn(c):
+        if near:
+
+            @pl.when(edge)
+            def _():
+                if c == 0:
+                    landed(near_dec, recv_nd, plane - 1).wait_recv()
+                    rate = near_dec[0]
+                    for t in range(1, plane):
+                        near_prod[t] = rate
+                        if t < plane - 1:
+                            rate = rate * near_dec[t]
+                landed(near_buf.at[c], recv_n1.at[c], plane - 1).wait_recv()
+                states = [near_buf[c, 0, p] for p in range(per)]
+                for t in range(1, plane):
+                    for p in range(per):
+                        near_chain[c, t, p] = states[p]
+                        if t < plane - 1:
+                            rate = near_dec[t, :, p * LANE : (p + 1) * LANE]
+                            states[p] = rate * states[p] + near_buf[c, t, p]
+                for t in range(1, plane):
+                    for q in range(plane):
+
+                        @pl.when(rank == q)
+                        def _():
+                            near_state(c, t, q).start()
+                            if c == 0:
+                                near_scale(t, q).start()
+
+    def near_drain(c):
+        if near:
+
+            @pl.when(ahead_of)
+            def _():
+                for q in range(plane):
+                    near_term(c, q).wait_send()
+                    if c == 0:
+                        near_decay(q).wait_send()
+
+            @pl.when(edge)
+            def _():
+                for t in range(1, plane):
+                    near_state(c, t, 0).wait_send()
+                    if c == 0:
+                        near_scale(t, 0).wait_send()
+
+    nearest = plane if near else 1
+
     def state_copy(e, dest, k):
         return pltpu.make_async_remote_copy(
             src_ref=chain_buf.at[e, dest],
@@ -197,7 +326,7 @@
         return True if swapped else n != other
 
     def sends_to(dest):
-        return n < cuts - 1 if swapped else jnp.logical_and(n != dest, n < cuts - 1)
+        return n < tail if swapped else jnp.logical_and(n != dest, n < cuts - 1)
 
     def chain_send(c, terms):
         for h in range(parts):
@@ -222,8 +351,10 @@
         def _():
             push(range(cols))
 
+        near_send(c)
+
     def wait_landed(buffer, recv, first, stop):
-        count = min(stop, cuts - 1) - first
+        count = min(stop, tail) - first
         if swapped:
             landed(buffer, recv, count).wait_recv()
         else:
@@ -255,13 +386,13 @@
                 state = origin_buf[h * high : (h + 1) * high]
                 for s in range(cuts):
                     chain_buf[e, s] = state
-                    if s > 0:
+                    if s >= nearest:
 
                         @pl.when(apart(s))
                         def _():
                             state_copy(e, s, piece).start()
 
-                    if s < cuts - 1:
+                    if s < tail:
                         if s % plane == 0:
                             group = recv1.at[e, s // plane]
                             wait_landed(gather_buf.at[e], group, s, s + plane)
@@ -274,14 +405,26 @@
         for e in blocks:
             for k in range(cols):
 
-                @pl.when(jnp.logical_and(apart(base + k), n > 0))
+                @pl.when(jnp.logical_and(apart(base + k), n >= nearest))
                 def _():
                     state_copy(e, 0, k).wait_recv()
 
-        return jnp.concatenate(
+        begin = jnp.concatenate(
             [jnp.concatenate([state_buf[e, k] for k in range(cols)], axis=1) for e in blocks],
             axis=0,
         )
+        if near:
+
+            @pl.when(behind)
+            def _():
+                for q in range(plane):
+                    near_state(c, 1, q).wait_recv()
+                    if c == 0:
+                        near_scale(1, q).wait_recv()
+
+            side = jnp.concatenate([side_buf[c, k] for k in range(cols)], axis=1)
+            begin = scale_buf[...] * begin + side
+        return begin
 
     def drain(c):
         for e in range(c * parts, (c + 1) * parts):
@@ -303,7 +446,7 @@
             if c == 0 and swapped:
                 origin_copy().wait_send()
             for e in range(c * parts, (c + 1) * parts):
-                for s in range(1, cuts):
+                for s in range(nearest, cuts):
 
                     @pl.when(apart(s))
                     def _():
@@ -389,7 +532,14 @@
         for copy in last_loads:
             copy.wait()
 
-    @pl.when(n == 0)
+    if near:
+
+        @pl.when(jnp.logical_not(behind))
+        def _():
+            side_buf[...] = jnp.zeros_like(side_buf)
+            scale_buf[...] = jnp.ones_like(scale_buf)
+
+    @pl.when(n < nearest)
     def _():
         for e in range((ITERS + 1) * parts):
             top = e % parts * high
@@ -402,7 +552,13 @@
         def _():
             pl.semaphore_wait(barrier, cuts - 1 + circ - 1)
 
-        @pl.when(jnp.logical_not(owner))
+        if near:
+
+            @pl.when(edge)
+            def _():
+                pl.semaphore_wait(barrier, cols + circ - 1 + plane - 1)
+
+        @pl.when(jnp.logical_not(jnp.logical_or(owner, edge) if near else owner))
         def _():
             pl.semaphore_wait(barrier, cols + circ - 1)
 
@@ -418,6 +574,7 @@
         @pl.when(owner)
         def _():
             origin_copy().start()
+
 
     with scope("port_t"):
         for g in range(circ):
@@ -445,6 +602,7 @@
         resp[ports : 2 * ports] = dot(resp[0:ports], pow1[...]).astype(BF16)
 
     with scope("turn0"):
+        near_turn(0)
         chain_turn(0)
 
     def beside(left, low, power):
@@ -512,27 +670,37 @@
     for iteration in range(ITERS):
         first = iteration * SWEEPS
         with scope("free"):
+            start_ref[...] = begin
             v0 = begin.astype(BF16)
-            outflow = dot(v0, port_t[...])
-            v1 = one_step(begin)
-            v2 = dot(v0, pow2[...])
-            v12 = jnp.concatenate([v1, v2], axis=0).astype(BF16)
+            if iteration == 0:
+                outflow = dot(v0, port_t[...])
+                v1 = one_step(begin)
+                v2 = dot(v0, pow2[...])
+            else:
+                v4 = dot(v0, pow4[...]).astype(BF16)
+                heard = dot(jnp.concatenate([v0, v4], axis=0), seen_t[...])
+                outflow = heard[0:scen, 0:width]
             if fused:
                 u_buf[iteration, me] = outflow
                 u_swaps[iteration].start()
             else:
                 exchange_start(first, outflow)
             if iteration == 0:
+                v12 = jnp.concatenate([v1, v2], axis=0).astype(BF16)
                 v34 = dot(v12, pow2[...])
                 v56 = dot(v34, pow2[...])
                 v78 = dot(v56, pow2[...])
                 v58 = jnp.concatenate([v56, v78], axis=0)
                 keep()
+                ending = free[last:]
                 seen = dot(free[...], port_t[...])
             else:
-                heard = dot(v12, seen_t[...])
-                pairs = [heard[:, k * width : (k + 1) * width] for k in range(steps // 2)]
-                seen = own_seen[...] + jnp.concatenate(pairs, axis=0)
+                slabs = [
+                    heard[r * scen : (r + 1) * scen, k * width : (k + 1) * width]
+                    for r in range(2)
+                    for k in range(1, steps // 2 + 1)
+                ]
+                seen = own_seen[...] + jnp.concatenate(slabs, axis=0)
         if fused:
             with scope("y_start"):
                 y_buf[iteration, me] = seen
@@ -545,9 +713,7 @@
                         take(peer(k))
             if iteration > 0:
                 with scope("later"):
-                    v34 = dot(v12, pow2[...])
-                    v58 = dot(jnp.concatenate([v12, v34.astype(BF16)], axis=0), pow4[...])
-                    free[last:] = own[last:] + v58[3 * scen :]
+                    ending = own[last:] + dot(v4, pow4[...])
             with scope("w_u"):
                 u_swaps[iteration].wait()
             with scope("ku"):
@@ -573,34 +739,43 @@
                 current = direct + dot(jnp.concatenate(columns, axis=1), k_me[...])
         else:
             if iteration > 0:
-                v34 = dot(v12, pow2[...])
-                v58 = dot(jnp.concatenate([v12, v34.astype(BF16)], axis=0), pow4[...])
-                free[last:] = own[last:] + v58[3 * scen :]
+                ending = own[last:] + dot(v4, pow4[...])
             current = exchange_end(first, scen)
             current = jnp.concatenate([current] * steps, axis=0)
             for sweep in range(1, SWEEPS):
                 exchange_start(first + sweep, seen + dot(by_lag(current), k_me[...]))
                 current = exchange_end(first + sweep, rows)
         with scope("final"):
-            final = free[last:] + dot(end_lags(current), resp[...])
+            final = ending + dot(end_lags(current), resp[...])
         with scope("send"):
-            chain_send(iteration + 1, final - dec_ref[...] * begin)
+            chain_send(iteration + 1, final - dec_ref[...] * start_ref[...])
         if iteration < ITERS - 1:
             with scope("pow4"):
                 product(pow4, pow2, pow2)
-                seen_t[:, width : 2 * width] = dot(pow2[...], port_t[...]).astype(BF16)
+            with scope("near"):
+                near_turn(iteration + 1)
+            with scope("seen"):
+                seen_t[:, width : 2 * width] = dot(pow1[...], port_t[...]).astype(BF16)
                 own_seen[...] = dot(own[...], port_t[...])
         else:
             with scope("wave"):
+                v1 = one_step(start_ref[...])
+                v2 = dot(start_ref[...], pow2[...])
+                v12 = jnp.concatenate([v1, v2], axis=0).astype(BF16)
+                v34 = dot(v12, pow2[...])
+                v58 = dot(jnp.concatenate([v12, v34.astype(BF16)], axis=0), pow4[...])
                 keep()
                 wave = free[...] + dot(by_lag(current), resp[...])
                 wave_ref[...] = wave.astype(BF16)
+            with scope("near"):
+                near_turn(iteration + 1)
         with scope("turn"):
             chain_turn(iteration + 1)
         if iteration < ITERS - 1:
             with scope("seen_t"):
-                half = seen_t[:, 0 : 2 * width]
-                seen_t[:, 2 * width : 4 * width] = dot(pow4[...], half).astype(BF16)
+                seen_t[:, 2 * width : 3 * width] = dot(pow2[...], port_t[...]).astype(BF16)
+                half = seen_t[:, width : 3 * width]
+                seen_t[:, 3 * width : 5 * width] = dot(pow2[...], half).astype(BF16)
         with scope("end"):
             begin = chain_end(iteration + 1)
     with scope("out"):
@@ -609,6 +784,7 @@
     with scope("drain"):
         for c in range(ITERS + 1):
             drain(c)
+            near_drain(c)
         if fused:
             k_swap.drain()
             for swap in u_swaps + y_swaps:
@@ -638,6 +814,8 @@
         rows = steps * scen
         cols = nodes // LANE
         high = scen
+        plane = math.gcd(cuts, 4)
+        per = max(cols // plane, 1)
         chains, swaps = (ITERS + 1) * (scen // high), ITERS * SWEEPS
         others = max(circ - 1, 1)
         fused = circ <= 2
@@ -665,7 +843,7 @@
                 square,
                 square,
                 square,
-                pltpu.VMEM((nodes, steps // 2 * circ * ports), BF16),
+                pltpu.VMEM((nodes, (steps // 2 + 1) * circ * ports), BF16),
                 pltpu.VMEM((steps * ports, nodes), BF16),
                 pltpu.VMEM((circ if fused else 1, span if fused else 8, circ * ports), F32),
                 pltpu.VMEM((circ * ports, steps * circ * ports) if fused else (16, LANE), BF16),
@@ -679,6 +857,12 @@
                 pltpu.VMEM((chains, cols, high, LANE), F32),
                 pltpu.VMEM((cuts, 1, LANE), F32),
                 pltpu.VMEM((scen, LANE), F32),
+                pltpu.VMEM((chains, plane, per, scen, LANE), F32),
+                pltpu.VMEM((chains, plane, per, scen, LANE), F32),
+                pltpu.VMEM((plane, 1, per * LANE), F32),
+                pltpu.VMEM((plane, 1, per * LANE), F32),
+                pltpu.VMEM((chains, cols, scen, LANE), F32),
+                pltpu.VMEM((1, nodes), F32),
                 pltpu.VMEM((ITERS, circ, scen, circ * ports), F32),
                 pltpu.VMEM((ITERS, circ, rows, circ * ports), F32),
                 pltpu.VMEM((1, 1, 8, LANE) if fused else (swaps, circ, rows, ports), F32),
@@ -691,6 +875,14 @@
                 dma(()),
                 dma(()),
                 dma(()),
+                dma((chains, plane)),
+                dma((chains,)),
+                dma((chains, plane)),
+                dma((chains, plane)),
+                dma((plane,)),
+                dma(()),
+                dma((plane,)),
+                dma((plane,)),
                 dma((others,)),
                 dma((circ,)),
                 dma((ITERS, others)),

time: 40 us -> 36.9 us (0.922)
  the two profiles are of different devices: /device:TPU:5 before, /device:TPU:25 now
where the time goes in v3:
time: 36.9 us; the launch traced here: 36.8 us
  Pallas kernels  36 us (98%)
  between operations  0.8 us (2%)
    pallas_call x1, Pallas kernels, shards(): pl.pallas_call(functools.partial(kernel, cuts, circ, steps, fused), out_s...  35.2 us
    pallas_call x1, Pallas kernels, shards(): pl.pallas_call(hand_over, out_shape=(jax.ShapeDtypeStruct(start.shape, F3...  0.74 us

profile of v3, /device:TPU:25, one launch (start us, length us, event | category | flops | bytes accessed | tf_op | source)
XLA Modules:
  0.0 36.8 jit_solution(11794382661040252517)
XLA Ops:
  0.6 35.2 %parareal.1 = (f32[16,1024]{1,0:T(8,128)S(1)}, bf16[128,1024]{1,0:T(8,128)(2,1)S(1)}) custom-call(bf16[128,1024]{1,0:T(8,128)(2,1)} %bitcast.12, bf16[1024,1024]{1,0:T(8,128)(2,1)} %bitcast.10, f32[1,1024]{1,0:T(1,128)} %bitcast.14, s32[1,4]{1,0:T(1,128)} %tgt_in.1, bf16[4,128,1024]{2,1,0:T(8,128)(2,1)} %bitcast.11, f32[1,1024]{1,0:T(1,128)} %bitcast.15, ...), custom_call_target="tpu_custom_call" | custom-call | tf_op jit(solution)/shard_map/parareal/pallas_call | solution.py:827
  35.9 0.7 %hand_over.1 = (f32[16,1024]{1,0:T(8,128)}, bf16[128,1024]{1,0:T(8,128)(2,1)}) custom-call(f32[16,1024]{1,0:T(8,128)S(1)} %get-tuple-element.6.start_in, bf16[128,1024]{1,0:T(8,128)(2,1)S(1)} %get-tuple-element.7.wave_in), custom_call_target="tpu_custom_call" | custom-call | tf_op jit(solution)/shard_map/hand_over/pallas_call | solution.py:909

commit v4 on v3

--- a/solution.py
+++ b/solution.py
@@ -168,8 +168,9 @@
         load(5, init_in, init_ref),
     ]
     strips = []
-    for c in range(cols):
-        at = pl.ds(c * LANE, LANE)
+    batch = math.gcd(cols, 4)
+    for c in range(cols // batch):
+        at = pl.ds(c * batch * LANE, batch * LANE)
         strips.append(pltpu.make_async_copy(inv_in.at[at], inv_ref.at[at], sem_inv.at[c]))
     for copy in first_loads + strips + last_loads:
         copy.start()
@@ -523,8 +524,9 @@
         factor = jnp.broadcast_to(mem_ref[...], (LANE, nodes)).T
     for c in range(cols):
         at = slice(c * LANE, (c + 1) * LANE)
-        with scope("w_inv"):
-            strips[c].wait()
+        if c % batch == 0:
+            with scope("w_inv"):
+                strips[c // batch].wait()
         turned = inv_ref[at, :].T
         inv_t[:, at] = turned
         pow1[:, at] = (turned.astype(F32) * factor).astype(BF16)
@@ -598,7 +600,7 @@
         resp[0:ports] = inv_t[0:ports]
 
     with scope("own1"):
-        own[scen:] = own[scen:] + one_step(own[: rows - scen])
+        own[scen:] = own[scen:] + dot(mem_ref[...] * own[: rows - scen], inv_t[...])
         resp[ports : 2 * ports] = dot(resp[0:ports], pow1[...]).astype(BF16)
 
     with scope("turn0"):

time: 36.9 us -> 36.9 us (level)
  no operation moved by 1% of the time
where the time goes in v4:
time: 36.9 us; the launch traced here: 36.8 us
  Pallas kernels  36 us (98%)
  between operations  0.8 us (2%)
    pallas_call x1, Pallas kernels, shards(): pl.pallas_call(functools.partial(kernel, cuts, circ, steps, fused), out_s...  35.2 us
    pallas_call x1, Pallas kernels, shards(): pl.pallas_call(hand_over, out_shape=(jax.ShapeDtypeStruct(start.shape, F3...  0.74 us

profile of v4, /device:TPU:25, one launch (start us, length us, event | category | flops | bytes accessed | tf_op | source)
XLA Modules:
  0.0 36.8 jit_solution(15148038208425618200)
XLA Ops:
  0.6 35.2 %parareal.1 = (f32[16,1024]{1,0:T(8,128)S(1)}, bf16[128,1024]{1,0:T(8,128)(2,1)S(1)}) custom-call(bf16[128,1024]{1,0:T(8,128)(2,1)} %bitcast.12, bf16[1024,1024]{1,0:T(8,128)(2,1)} %bitcast.10, f32[1,1024]{1,0:T(1,128)} %bitcast.14, s32[1,4]{1,0:T(1,128)} %tgt_in.1, bf16[4,128,1024]{2,1,0:T(8,128)(2,1)} %bitcast.11, f32[1,1024]{1,0:T(1,128)} %bitcast.15, ...), custom_call_target="tpu_custom_call" | custom-call | tf_op jit(solution)/shard_map/parareal/pallas_call | solution.py:829
  35.9 0.7 %hand_over.1 = (f32[16,1024]{1,0:T(8,128)}, bf16[128,1024]{1,0:T(8,128)(2,1)}) custom-call(f32[16,1024]{1,0:T(8,128)S(1)} %get-tuple-element.6.start_in, bf16[128,1024]{1,0:T(8,128)(2,1)S(1)} %get-tuple-element.7.wave_in), custom_call_target="tpu_custom_call" | custom-call | tf_op jit(solution)/shard_map/hand_over/pallas_call | solution.py:911
